TPU v7x, 8 devices: a whole 2x2x1 slice. The times are simulated.
8 devices in a mesh: dp: 8 (over z, y, x, core).
Axes of the slice: x: 2, y: 2, z: 1, core: 2. Of those that a mesh axis runs over, the one named last changes fastest.
Arguments:
- grad_wq: bfloat16 [8, 2, 896, 896], P('dp')
- grad_wk: bfloat16 [8, 2, 896, 128], P('dp')
- grad_wv: bfloat16 [8, 2, 896, 128], P('dp')
- grad_wo: bfloat16 [8, 2, 896, 896], P('dp')
- grad_gate: bfloat16 [8, 2, 896, 4864], P('dp')
- grad_up: bfloat16 [8, 2, 896, 4864], P('dp')
- grad_down: bfloat16 [8, 2, 4864, 896], P('dp')
- grad_attn_norm: bfloat16 [8, 2, 896], P('dp')
- grad_mlp_norm: bfloat16 [8, 2, 896], P('dp')
- grad_final_norm: bfloat16 [8, 896], P('dp')
- master: float32 [29824000], P('dp')
- exp_avg: float32 [29824000], P('dp')
- exp_avg_sq: float32 [29824000], P('dp')
- learn_rate: float32 [], replicated
Outputs:
- output 1: float32 [29824000], P('dp')
- output 2: float32 [29824000], P('dp')
- output 3: float32 [29824000], P('dp')
- output 4: bfloat16 [2, 896, 896], replicated
- output 5: bfloat16 [2, 896, 128], replicated
- output 6: bfloat16 [2, 896, 128], replicated
- output 7: bfloat16 [2, 896, 896], replicated
- output 8: bfloat16 [2, 896, 4864], replicated
- output 9: bfloat16 [2, 896, 4864], replicated
- output 10: bfloat16 [2, 4864, 896], replicated
- output 11: bfloat16 [2, 896], replicated
- output 12: bfloat16 [2, 896], replicated
- output 13: bfloat16 [896], replicated
- output 14: float32 [], replicated
All inputs are finite; a program needn't handle non-finite values.
Results may differ from a plain program's by a relative error of at most 0.001.
Values sent between devices are 32-bit elements.
A program may use at most 1 GiB of HBM per device.

v0:
```python
import functools
import math
import jax
import jax.numpy as jnp
from jax import lax
from jax.experimental import pallas as pl
from jax.experimental.pallas import tpu as pltpu
from jax.sharding import PartitionSpec as P

BETA_ONE = 0.9
BETA_TWO = 0.95
ADAM_EPS = 1e-8
WEIGHT_DECAY = 0.1
MAX_NORM = 1.0
CLIP_EPS = 1e-6
STEP = 4
BIAS_ONE = 1.0 - BETA_ONE ** STEP
BIAS_TWO = 1.0 - BETA_TWO ** STEP

MESH = pl.DeviceIdType.MESH
F32 = jnp.float32
BF16 = jnp.bfloat16
LANES = 128

LAYERS, D, KV, FF = 2, 896, 128, 4864
SHAPES = [(LAYERS, D, D), (LAYERS, D, KV), (LAYERS, D, KV), (LAYERS, D, D), (LAYERS, D, FF), (LAYERS, D, FF), (LAYERS, FF, D)]
GAINS = [(LAYERS, D), (LAYERS, D), (1, D)]
TAIL = 40
HALVES, TENSORS, COLUMNS = range(2), range(7), range(7)
NAMES_ROWS = [math.prod(s[:-1]) for s in SHAPES]
WIDTHS = [s[-1] // LANES for s in SHAPES]
OFFSETS = [sum(r * w for r, w in zip(NAMES_ROWS[:t], WIDTHS[:t])) for t in TENSORS]
BLOCK_ROWS = [448, 1792, 1792, 448, 128, 128, 608]
MATRIX_ROWS = 232960
FLAT_ROWS = 233000
SEG = 29125
NDEV = 8

WIDTH_ORDER = (38, 7, 1)
GROUPS = {38: (16,), 7: (16, 32, 64), 1: (16, 128, 256)}
STAGE_ROWS = max(br * WIDTHS[t] for t, br in enumerate(BLOCK_ROWS))


def split(refs, counts):
    refs = list(refs)
    return [[refs.pop(0) for _ in range(n)] for n in counts]


ANY = pl.BlockSpec(memory_space=pl.ANY)
VMEM_SPEC = pl.BlockSpec(memory_space=pltpu.VMEM)
SMEM_SPEC = pl.BlockSpec(memory_space=pltpu.SMEM)
DMA = pltpu.SemaphoreType.DMA
VMEM_LIMIT = 63 * 1024 * 1024
COST = pl.CostEstimate(flops=2 * 10 ** 8, bytes_accessed=10 ** 8, transcendentals=0)


def tile_scratch(slots, rows):
    return [pltpu.VMEM((slots, r, w * LANES), BF16) for r, w in zip(rows, WIDTH_ORDER)]


def width_slot(width):
    return WIDTH_ORDER.index(width)


def row_group(rows, width):
    return max(g for g in GROUPS[width] if rows % g == 0)


PIECE = 912
PIECES = 32
LATE_FIRST, LATE_END = 25, 31
LATE_ROWS = PIECE * (LATE_END - LATE_FIRST) + 16
PIECE_LAST = SEG - (PIECES - 1) * PIECE
HALF = (PIECES - LATE_END + LATE_FIRST) // 2
LATE_HALF = (LATE_ROWS + 16) // 2
LATE_STARTS = (0, LATE_ROWS - LATE_HALF)
LATE_RANGES = [((SEG * s + PIECE * LATE_FIRST) // 8 * 8, -(-(SEG * s + PIECE * LATE_END) // 8) * 8) for s in range(NDEV)]


def unpack_blocks():
    early, late = [], []
    for t in TENSORS:
        w, offset, total = WIDTHS[t], OFFSETS[t], NAMES_ROWS[t]
        cuts = {0, total}
        spans = []
        for low, high in LATE_RANGES:
            first = max(0, (low - offset) // (16 * w) * 16)
            end = min(total, -(-(high - offset) // (16 * w)) * 16)
            if first < end:
                spans.append((first, end))
                cuts |= {first, end}
        cuts = sorted(cuts)
        for begin, end in zip(cuts[:-1], cuts[1:]):
            is_late = any(first <= begin and end <= last for first, last in spans)
            count = -(-(end - begin) // BLOCK_ROWS[t])
            step = -(-(end - begin) // (16 * count)) * 16
            for row in range(begin, end, step):
                rows = min(step, end - row)
                low, high = offset + row * w, offset + (row + rows) * w
                middles = [l + LATE_STARTS[1] for l, _ in LATE_RANGES]
                edges = sorted({low, high} | {e for r in LATE_RANGES + [middles] for e in r if low < e < high})
                sources = []
                for e0, e1 in zip(edges[:-1], edges[1:]):
                    seg = [s for s, (l, h) in enumerate(LATE_RANGES) if l <= e0 and e1 <= h]
                    source = None
                    start = e0
                    if seg:
                        start = e0 - SEG * seg[0] - PIECE * LATE_FIRST + 8
                        half = int(e0 >= middles[seg[0]])
                        source, start = (seg[0], half), start - LATE_STARTS[half]
                    sources.append((source, start, e0 - low, e1 - e0))
                (late if is_late else early).append((t, row, rows, sources))
    return early, late


EARLY_BLOCKS, LATE_BLOCKS = unpack_blocks()
LATE_TENSORS = sorted({t for t, _, _, _ in LATE_BLOCKS})
SLOTS = 4


def unpack_body(blocks, flat, lates, outs, tiles, stage, in_sem, out_sem, wanted=None):
    def when(b):
        return pl.when(wanted(b)) if wanted else lambda f: f()

    def loads(b, start=True):
        for n, (source, row, to, rows) in enumerate(blocks[b][3]):
            def copy(ref):
                return pltpu.make_async_copy(ref.at[pl.ds(row, rows), 0], stage.at[b % SLOTS, pl.ds(to, rows)], in_sem.at[b % SLOTS, n])

            if not start:
                copy(flat).wait()
            elif source is None:
                copy(flat).start()
            else:
                for relation, halves in lates.items():
                    @pl.when(lax.bitwise_xor(lax.axis_index("dp"), source[0]) == relation)
                    def _():
                        copy(halves[source[1]]).start()

    def store(b):
        t, row, rows, _ = blocks[b]
        return pltpu.make_async_copy(tiles[width_slot(WIDTHS[t])].at[b % SLOTS, pl.ds(0, rows)], outs[t].at[pl.ds(row, rows)], out_sem.at[b % SLOTS])

    for b in range(min(SLOTS, len(blocks))):
        when(b)(lambda: loads(b))
    yield
    for b, (t, row, rows, _) in enumerate(blocks):
        w = WIDTHS[t]
        tile = tiles[width_slot(w)]
        group = row_group(rows, w)
        if b >= SLOTS:
            when(b - SLOTS)(lambda: store(b - SLOTS).wait())

        @when(b)
        def _():
            loads(b, start=False)

            @pl.loop(0, rows // group)
            def _(i):
                for j in range(w):
                    if w == 1:
                        block = stage[b % SLOTS, pl.ds(pl.multiple_of(i * group, 16), group), :]
                    else:
                        block = stage[b % SLOTS, pl.ds(i * (group * w) + j, group, stride=w), :]
                    tile[b % SLOTS, pl.ds(pl.multiple_of(i * group, 16), group), pl.ds(j * LANES, LANES)] = block.astype(BF16)

            store(b).start()

        if b + SLOTS < len(blocks):
            when(b + SLOTS)(lambda: loads(b + SLOTS))
    for b in range(max(0, len(blocks) - SLOTS), len(blocks)):
        when(b)(lambda: store(b).wait())


UNPACK_SCRATCH = tile_scratch(SLOTS, (128, 608, 1792)) + [pltpu.VMEM((SLOTS, STAGE_ROWS, LANES), F32)]
TENSOR_TYPES = [jax.ShapeDtypeStruct((r, w * LANES), BF16) for r, w in zip(NAMES_ROWS, WIDTHS)]


def unpack_early_kernel(tensors, flat, *refs):
    gains = len(refs) - len(tensors) - 8
    outs, norms, tiles, (stage, tail, in_sem, out_sem, tail_sem) = split(refs, (len(tensors), gains, 3, 5))
    tail_copy = pltpu.make_async_copy(flat.at[pl.ds(MATRIX_ROWS, TAIL), 0], tail, tail_sem)
    tail_copy.start()
    work = unpack_body([b for b in EARLY_BLOCKS if b[0] in tensors], flat, None, dict(zip(tensors, outs)), tiles, stage, in_sem, out_sem)
    next(work)
    tail_copy.wait()
    base = 0
    for n in norms:
        if n.ndim == 1:
            n[...] = jnp.concatenate([tail[base + j, :] for j in COLUMNS]).astype(BF16)
            continue
        for j in COLUMNS:
            lines = [tail[pl.ds(base + j + 7 * layer, 1), :] for layer in range(n.shape[0])]
            n[:, pl.ds(j * LANES, LANES)] = jnp.concatenate(lines, axis=0).astype(BF16)
        base += 7 * n.shape[0]
    for _ in work:
        pass


def unpack_early(flat, tensors, gains):
    return pl.pallas_call(
        functools.partial(unpack_early_kernel, tensors),
        name="unpack_early",
        out_shape=[TENSOR_TYPES[t] for t in tensors] + [jax.ShapeDtypeStruct(s, BF16) for s in gains],
        in_specs=[ANY],
        out_specs=[ANY] * len(tensors) + [VMEM_SPEC] * len(gains),
        scratch_shapes=UNPACK_SCRATCH + [pltpu.VMEM((TAIL, LANES), F32), DMA((SLOTS, 4)), DMA((SLOTS,)), DMA],
        compiler_params=pltpu.CompilerParams(vmem_limit_bytes=VMEM_LIMIT),
        cost_estimate=COST,
    )(flat)


def unpack_late_kernel(relations, flat, *refs):
    count = len(LATE_TENSORS)
    lates, _, outs, tiles, (stage, in_sem, out_sem) = split(refs, (2 * len(relations), count, count, 3, 3))
    lates = dict(zip(relations, zip(lates[::2], lates[1::2])))

    def wanted(b):
        seg = [source[0] for source, _, _, _ in LATE_BLOCKS[b][3] if source][0]
        relation = lax.bitwise_xor(lax.axis_index("dp"), seg)
        return jnp.logical_and(relation >= relations[0], relation <= relations[-1])

    for _ in unpack_body(LATE_BLOCKS, flat, lates, dict(zip(LATE_TENSORS, outs)), tiles, stage, in_sem, out_sem, wanted):
        pass


def unpack_late(flat, lates, params):
    count = len(LATE_TENSORS)
    relations = sorted(lates)
    lates = [a for r in relations for a in lates[r]]
    outs = pl.pallas_call(
        functools.partial(unpack_late_kernel, relations),
        name="unpack_late",
        out_shape=[TENSOR_TYPES[t] for t in LATE_TENSORS],
        in_specs=[ANY] * (1 + len(lates) + count),
        out_specs=[ANY] * count,
        input_output_aliases={1 + len(lates) + n: n for n in range(count)},
        scratch_shapes=UNPACK_SCRATCH + [DMA((SLOTS, 4)), DMA((SLOTS,))],
        compiler_params=pltpu.CompilerParams(vmem_limit_bytes=VMEM_LIMIT),
        cost_estimate=COST,
    )(flat, *lates, *[params[t] for t in LATE_TENSORS])
    return {**params, **dict(zip(LATE_TENSORS, outs))}


def neighbours():
    me = lax.axis_index("dp")
    core, x, y = lax.rem(me, 2), lax.rem(me // 2, 2), me // 4
    other = 1 - 2 * core
    step_x, step_y = 2 - 4 * x, 4 - 8 * y
    return me, other, me + step_x, me + step_y, me + step_x + step_y


CHUNKS = 16
RS_ROWS = 911
RS_HALF_START = SEG - CHUNKS * RS_ROWS
UNITS = 4
UNIT_CHUNKS = CHUNKS // UNITS
KIND_D, KIND_N, KIND_S, KIND_O = range(4)
CHIP_D, CHIP_X, CHIP_Y, CHIP_OWN = range(4)
UNIT_ROWS = UNIT_CHUNKS * RS_ROWS
MARGIN = 16 * 38
PACK_ROWS = {38: 112, 7: 608, 1: 896}
PACK_STAGE = 112 * 38
PACK_SLOTS = 3


def pack_blocks(chip, unit):
    blocks = []
    for parity in HALVES:
        for h in HALVES:
            begin = SEG * (2 * chip + parity) + RS_HALF_START * h + UNIT_ROWS * unit
            for t in TENSORS:
                w, offset, total = WIDTHS[t], OFFSETS[t], NAMES_ROWS[t]
                low, high = max(begin, offset), min(begin + UNIT_ROWS, offset + total * w)
                if low >= high:
                    continue
                first = (low - offset) // (16 * w) * 16
                end = -(-(high - offset) // (16 * w)) * 16
                step = -(-(end - first) // (16 * -(-(end - first) // PACK_ROWS[w]))) * 16
                for row in range(first, end, step):
                    blocks.append((t, row, min(step, end - row), parity, h, offset + row * w - begin + MARGIN))
    return blocks


def reduce_kernel(*refs):
    (grads, norms, (g_out, norm_out, flat, land_p, land_d, land_n),
     (mine, part, first, land_s, sums, g_buf, ss, ss_all), tiles, (stage, tail),
     (p_send, p_recv, i_send, i_recv, load_sem, g_sem, ss_send, ss_recv, in_sem, out_sem, tail_sem)) = split(refs, (7, 3, 6, 8, 3, 2, 11))
    me, other, dev_x, dev_y, _ = neighbours()
    core, x, y = lax.rem(me, 2), lax.rem(me // 2, 2), me // 4
    barrier = pltpu.get_barrier_semaphore()
    for d in range(1, NDEV):
        pl.semaphore_signal(barrier, inc=1, device_id=(lax.rem(me + d, NDEV),), device_id_type=MESH)

    tail[...] = jnp.zeros_like(tail)
    line = 0
    for n in norms:
        for layer in range(n.shape[0]):
            for j in COLUMNS:
                tail[pl.ds(line, 1), :] = n[pl.ds(layer, 1), pl.ds(j * LANES, LANES)].astype(F32)
                line += 1

    def pack(place, chip, unit):
        blocks = pack_blocks(chip, unit)

        def load(b):
            t, row, rows = blocks[b][:3]
            return pltpu.make_async_copy(grads[t].at[pl.ds(row, rows)], tiles[width_slot(WIDTHS[t])].at[b % PACK_SLOTS, pl.ds(0, rows)], in_sem.at[b % PACK_SLOTS])

        def store(b):
            t, _, rows, parity, h, to = blocks[b]
            size = rows * WIDTHS[t]
            return pltpu.make_async_copy(stage.at[b % PACK_SLOTS, pl.ds(0, size)], flat.at[place, unit, parity, h, pl.ds(to, size), 0], out_sem.at[b % PACK_SLOTS])

        for b in range(PACK_SLOTS):
            load(b).start()
        tail_copies = [pltpu.make_async_copy(tail, flat.at[place, unit, 1, 1, pl.ds(MARGIN + UNIT_ROWS - TAIL, TAIL), 0], tail_sem)
                       for _ in range(chip * unit // (3 * UNITS - 3))]
        for copy in tail_copies:
            copy.start()
        for b, block in enumerate(blocks):
            t, rows = block[0], block[2]
            w = WIDTHS[t]
            tile = tiles[width_slot(w)]
            group = row_group(rows, w)
            load(b).wait()
            if b >= PACK_SLOTS:
                store(b - PACK_SLOTS).wait()

            @pl.loop(0, rows // group)
            def _(i):
                for j in range(w):
                    values = tile[b % PACK_SLOTS, pl.ds(pl.multiple_of(i * group, 16), group), pl.ds(j * LANES, LANES)].astype(F32)
                    if w == 1:
                        stage[b % PACK_SLOTS, pl.ds(pl.multiple_of(i * group, 16), group), :] = values
                    else:
                        stage[b % PACK_SLOTS, pl.ds(i * (group * w) + j, group, stride=w), :] = values

            store(b).start()
            if b + PACK_SLOTS < len(blocks):
                load(b + PACK_SLOTS).start()
        for b in range(len(blocks) - PACK_SLOTS, len(blocks)):
            store(b).wait()
        for copy in tail_copies:
            copy.wait()

    def place_of(kind, h):
        return ((CHIP_D, CHIP_D), (CHIP_X, CHIP_Y), (CHIP_Y, CHIP_X), (CHIP_OWN, CHIP_OWN))[kind][h]

    def chunk(kind, h, i, parity):
        return flat.at[place_of(kind, h), i // UNIT_CHUNKS, parity, h, pl.ds(MARGIN + RS_ROWS * lax.rem(i, UNIT_CHUNKS), RS_ROWS)]

    def start_row(h, i):
        return RS_HALF_START * h + RS_ROWS * i

    def partner_copy(kind, h, i):
        return pltpu.make_async_remote_copy(
            src_ref=chunk(kind, h, i, 1 - core), dst_ref=land_p.at[kind, h, i],
            send_sem=p_send.at[kind, h, i], recv_sem=p_recv.at[kind, h, i],
            device_id=(me + other,), device_id_type=MESH)

    def link_copy(kind, h, i):
        land = land_s.at[h, i] if kind == KIND_S else (land_d, land_n)[kind].at[h, i, pl.ds(0, RS_ROWS), 0]
        to = ((dev_x, dev_y), (dev_x, dev_y), (dev_y, dev_x))[kind][h]
        return pltpu.make_async_remote_copy(
            src_ref=sums.at[kind % 2, h, i], dst_ref=land,
            send_sem=i_send.at[kind, h, i], recv_sem=i_recv.at[kind, h, i],
            device_id=(to,), device_id_type=MESH)

    def load_mine(kind, h, i):
        return pltpu.make_async_copy(chunk(kind, h, i, core).at[:, 0], mine.at[h], load_sem.at[0, h])

    def load_part(kind, h, i):
        return pltpu.make_async_copy(land_p.at[kind, h, i, pl.ds(0, RS_ROWS), 0], part.at[h], load_sem.at[1, h])

    def load_link(land, buf, n, h, i):
        return pltpu.make_async_copy(land.at[h, i, pl.ds(0, RS_ROWS), 0], buf.at[h], load_sem.at[n, h])

    def store_g(h, i):
        return pltpu.make_async_copy(g_buf.at[h], g_out.at[pl.ds(start_row(h, i), RS_ROWS), 0], g_sem.at[h])

    def exchange(kinds, begin, end):
        @pl.loop(begin, end)
        def _(i):
            for kind in kinds:
                for h in HALVES:
                    partner_copy(kind, h, i).start()

    def send(kind, begin, end):
        @pl.loop(begin, end)
        def _(i):
            for h in HALVES:
                load_mine(kind, h, i).start()
            for h in HALVES:
                partner_copy(kind, h, i).wait_recv()
                load_part(kind, h, i).start()
                if kind == KIND_S:
                    link_copy(KIND_D, h, i).wait_recv()
                    load_link(land_d, first, 2, h, i).start()
            for h in HALVES:
                load_mine(kind, h, i).wait()
                load_part(kind, h, i).wait()
                total = mine[h] + part[h]
                if kind == KIND_S:
                    load_link(land_d, first, 2, h, i).wait()
                    total = total + first[h]
                    link_copy(KIND_D, h, i).wait_send()
                sums[kind % 2, h, i] = total
                link_copy(kind, h, i).start()

    @pl.loop(0, 4 * UNITS)
    def _(n):
        place, unit = n // UNITS, lax.rem(n, UNITS)
        flip_x, flip_y = 1 - place // 2, 1 - lax.rem(place, 2)
        chip = (x + flip_x * (1 - 2 * x)) + 2 * (y + flip_y * (1 - 2 * y))
        for case in range(4 * UNITS):
            @pl.when(UNITS * chip + unit == case)
            def _():
                pack(place, case // UNITS, case % UNITS)

        @pl.when(n == 0)
        def _():
            pl.semaphore_wait(barrier, NDEV - 1)

        @pl.when(n < UNITS)
        def _():
            exchange((KIND_D,), UNIT_CHUNKS * unit, UNIT_CHUNKS * unit + UNIT_CHUNKS)
            send(KIND_D, UNIT_CHUNKS * unit, UNIT_CHUNKS * unit + UNIT_CHUNKS)

        @pl.when(n == 3 * UNITS - 1)
        def _():
            exchange((KIND_N, KIND_S), 0, CHUNKS)
            send(KIND_N, 0, CHUNKS)

    exchange((KIND_O,), 0, CHUNKS)
    send(KIND_S, 0, CHUNKS)

    def last(i, acc):
        for h in HALVES:
            for kind in (KIND_D, KIND_N, KIND_S):
                partner_copy(kind, h, i).wait_send()
            link_copy(KIND_N, h, i).wait_send()

            @pl.when(i > 0)
            def _():
                partner_copy(KIND_O, h, i - 1).wait_send()
                link_copy(KIND_S, h, i - 1).wait_send()

        for h in HALVES:
            load_mine(KIND_O, h, i).start()
            partner_copy(KIND_O, h, i).wait_recv()
            load_part(KIND_O, h, i).start()
        for h in HALVES:
            link_copy(KIND_N, h, i).wait_recv()
            load_link(land_n, first, 2, h, i).start()
        for h in HALVES:
            load_mine(KIND_O, h, i).wait()
            load_part(KIND_O, h, i).wait()
            load_link(land_n, first, 2, h, i).wait()
            link_copy(KIND_S, h, i).wait_recv()

            @pl.when(i > 0)
            def _():
                store_g(h, i - 1).wait()

            g = ((mine[h] + part[h]) + (first[h] + land_s[h, i])) * (1.0 / NDEV)
            g_buf[h] = g
            store_g(h, i).start()
            square = g * g
            if h == 1:
                row = lax.broadcasted_iota(jnp.int32, (RS_ROWS, LANES), 0) + RS_ROWS * i
                square = jnp.where(row >= CHUNKS * RS_ROWS - RS_HALF_START, square, 0.0)
            acc = acc + jnp.sum(square, axis=0, keepdims=True)
        return acc

    acc = lax.fori_loop(0, CHUNKS, last, jnp.zeros((1, LANES), F32))
    ss[...] = jnp.broadcast_to(acc, (8, LANES))

    for h in HALVES:
        partner_copy(KIND_O, h, CHUNKS - 1).wait_send()
        link_copy(KIND_S, h, CHUNKS - 1).wait_send()
    store_g(0, CHUNKS - 1).wait()

    def norm_copy(d):
        return pltpu.make_async_remote_copy(
            src_ref=ss, dst_ref=ss_all.at[d], send_sem=ss_send.at[d], recv_sem=ss_recv.at[d],
            device_id=(lax.rem(me + d, NDEV),), device_id_type=MESH)

    for d in range(1, NDEV):
        norm_copy(d).start()
    store_g(1, CHUNKS - 1).wait()
    ss_all[0] = ss[...]
    for d in range(1, NDEV):
        norm_copy(d).wait()
    total = jnp.zeros((8, LANES), F32)
    for dev in range(NDEV):
        total = total + ss_all[lax.rem(me - dev + NDEV, NDEV)]
    norm_out[...] = jnp.broadcast_to(jnp.sqrt(jnp.sum(total, axis=1, keepdims=True)), (8, LANES))


def reduce_grads(grads, norms):
    land = jax.ShapeDtypeStruct((2, CHUNKS, RS_ROWS, 1, LANES), F32)
    land_p = jax.ShapeDtypeStruct((4, 2, CHUNKS, RS_ROWS, 1, LANES), F32)
    flat = jax.ShapeDtypeStruct((4, UNITS, 2, 2, UNIT_ROWS + 2 * MARGIN, 1, LANES), F32)
    buf = pltpu.VMEM((2, RS_ROWS, LANES), F32)
    partner, link, pair, all_devs, slots = DMA((4, 2, CHUNKS)), DMA((3, 2, CHUNKS)), DMA((2,)), DMA((NDEV,)), DMA((PACK_SLOTS,))
    outs = pl.pallas_call(
        reduce_kernel,
        name="reduce_grads",
        out_shape=[jax.ShapeDtypeStruct((SEG, 1, LANES), F32), jax.ShapeDtypeStruct((8, LANES), F32), flat, land_p, land, land],
        in_specs=[ANY] * 7 + [VMEM_SPEC] * 3,
        out_specs=[ANY, VMEM_SPEC] + [ANY] * 4,
        scratch_shapes=[buf] * 3 + [pltpu.VMEM((2, CHUNKS, RS_ROWS, LANES), F32), pltpu.VMEM((2, 2, CHUNKS, RS_ROWS, LANES), F32), buf, pltpu.VMEM((8, LANES), F32), pltpu.VMEM((NDEV, 8, LANES), F32)]
        + tile_scratch(PACK_SLOTS, PACK_ROWS.values()) + [pltpu.VMEM((PACK_SLOTS, PACK_STAGE, LANES), F32), pltpu.VMEM((TAIL, LANES), F32)]
        + [partner, partner, link, link, DMA((4, 2)), pair, all_devs, all_devs, slots, slots, DMA],
        compiler_params=pltpu.CompilerParams(collective_id=0, has_side_effects=True, vmem_limit_bytes=VMEM_LIMIT),
        cost_estimate=COST,
    )(*grads, *norms)
    return outs[0], outs[1]


def adam_rows(g, m, v, p, norm_row, lr, decay):
    clip = jnp.minimum(1.0, MAX_NORM / (norm_row + CLIP_EPS))
    clipped = clip * g
    new_m = BETA_ONE * m + (1.0 - BETA_ONE) * clipped
    new_v = BETA_TWO * v + (1.0 - BETA_TWO) * clipped * clipped
    adam_dir = (new_m * (1.0 / BIAS_ONE)) / (jnp.sqrt(new_v * (1.0 / BIAS_TWO)) + ADAM_EPS)
    decay_term = jnp.where(decay, WEIGHT_DECAY * p, 0.0)
    return p - lr * (decay_term + adam_dir), new_m, new_v


STATE_ROWS = PIECE
STATE_COUNT = SEG // STATE_ROWS
STATE_LAST = SEG - STATE_COUNT * STATE_ROWS
STATE_SLOTS = 4
SUB = 152


def decay_rows(me, start, rows):
    return lax.broadcasted_iota(jnp.int32, (rows, LANES), 0) + (SEG * me + start) < MATRIX_ROWS


def gather_kernel(g, m, v, p, norm, lr, full, late_a, late_b, gb, mb, vb, pb, new_p, late_p,
                  load_sem, own_sem, late_sem, own_send, own_recv, fwd_send, fwd_recv, p_send, p_recv):
    me, other, dev_x, dev_y, dev_d = neighbours()
    partner = me + other
    barrier = pltpu.get_barrier_semaphore()
    for dev in (partner, dev_x, dev_y):
        pl.semaphore_signal(barrier, inc=1, device_id=(dev,), device_id_type=MESH)
    to = (dev_x, dev_y, partner)
    sources = (me, dev_x, dev_y, dev_d)

    def is_last(h, i):
        return h == 1 and isinstance(i, int) and i == HALF - 1

    def start_row(h, i):
        return PIECE * (PIECES - 1) if is_last(h, i) else PIECE * (HALF * h + i)

    def size(h, i):
        return PIECE_LAST if is_last(h, i) else PIECE

    def rows_of(dev, h, i):
        return full.at[pl.ds(SEG * dev + start_row(h, i), size(h, i)), 0]

    def loads(h, i):
        return loads_at(h, start_row(h, i), size(h, i))

    def loads_at(h, start, rows):
        start = pl.multiple_of(start, 8)
        copies = [pltpu.make_async_copy(g.at[pl.ds(start, rows), 0], gb.at[h, pl.ds(0, rows)], load_sem.at[0, h])]
        for n, (src, buf) in enumerate(((m, mb), (v, vb), (p, pb))):
            copies.append(pltpu.make_async_copy(src.at[pl.ds(start, rows)], buf.at[h, pl.ds(0, rows)], load_sem.at[n + 1, h]))
        return copies

    def own_copy(n, h, i):
        return pltpu.make_async_remote_copy(
            src_ref=new_p.at[h, i, pl.ds(0, size(h, i))], dst_ref=rows_of(me, h, i),
            send_sem=own_send.at[n, h, i], recv_sem=own_recv.at[n, h, i], device_id=(to[n],), device_id_type=MESH)

    def own_store(h, i):
        return pltpu.make_async_copy(new_p.at[h, i, pl.ds(0, size(h, i))], rows_of(me, h, i), own_sem.at[h, i])

    def forward(h, i):
        src = rows_of((dev_y, dev_x)[h], h, i)
        return pltpu.make_async_remote_copy(
            src_ref=src, dst_ref=src, send_sem=fwd_send.at[h, i], recv_sem=fwd_recv.at[h, i],
            device_id=((dev_x, dev_y)[h],), device_id_type=MESH)

    def arrival(n, h, i):
        src = rows_of((dev_x, dev_y, partner)[n], h, i)
        return pltpu.make_async_remote_copy(
            src_ref=src, dst_ref=src, send_sem=own_send.at[n, h, i], recv_sem=own_recv.at[n, h, i],
            device_id=(to[n],), device_id_type=MESH)

    def forward_arrival(h, i):
        src = rows_of(dev_d, h, i)
        return pltpu.make_async_remote_copy(
            src_ref=src, dst_ref=src, send_sem=fwd_send.at[h, i], recv_sem=fwd_recv.at[h, i],
            device_id=((dev_x, dev_y)[h],), device_id_type=MESH)

    def partner_copy(q, h, i):
        src = rows_of(sources[q], h, i)
        return pltpu.make_async_remote_copy(
            src_ref=src, dst_ref=src, send_sem=p_send.at[q - 1, h, i], recv_sem=p_recv.at[q - 1, h, i],
            device_id=(partner,), device_id_type=MESH)

    def partner_arrival(q, h, i):
        src = rows_of(sources[q] + other, h, i)
        return pltpu.make_async_remote_copy(
            src_ref=src, dst_ref=src, send_sem=p_send.at[q - 1, h, i], recv_sem=p_recv.at[q - 1, h, i],
            device_id=(partner,), device_id_type=MESH)

    def each(body):
        @pl.loop(0, HALF - 1)
        def _(i):
            body(i)

        body(HALF - 1)

    norm_row = norm[0:1, :]
    for h in HALVES:
        for copy in loads(h, 0):
            copy.start()
    pl.semaphore_wait(barrier, 3)

    def compute(h, out, first):
        @pl.loop(0, PIECE // SUB)
        def _(s):
            start = pl.multiple_of(s * SUB, 8)
            sub = pl.ds(start, SUB)
            out[sub] = adam_rows(gb[h, sub], mb[h, sub], vb[h, sub], pb[h, sub], norm_row, lr[0], decay_rows(me, first + start, SUB))[0]

    def update(i):
        for h in HALVES:
            for copy in loads(h, i):
                copy.wait()

            compute(h, new_p.at[h, i], start_row(h, i))
            for n in ((1, 0, 2) if h == 0 else (0, 1, 2)):
                own_copy(n, h, i).start()
            own_store(h, i).start()
            if isinstance(i, int):
                continue
            for last in (False, True):
                @pl.when((i == HALF - 2) == last)
                def _():
                    for copy in loads(h, HALF - 1 if last else i + 1):
                        copy.start()

    each(update)

    late_copies = []

    def late_store(src, row, rows, to):
        for out, start in zip((late_a, late_b), LATE_STARTS):
            low, high = max(to, start), min(to + rows, start + LATE_HALF)
            if low < high:
                late_copies.append(pltpu.make_async_copy(src.at[pl.ds(row + low - to, high - low)], out.at[pl.ds(low - start, high - low), 0], late_sem.at[len(late_copies)]))
                late_copies[-1].start()

    late_store(new_p.at[1, HALF - 2], PIECE - 8, 8, 0)
    late_store(new_p.at[1, HALF - 1], 0, 8, LATE_ROWS - 8)
    for j in range(LATE_END - LATE_FIRST):
        first = PIECE * (LATE_FIRST + j)
        for copy in loads_at(j % 2, first, PIECE):
            copy.start()
        for copy in loads_at(j % 2, first, PIECE):
            copy.wait()
        compute(j % 2, late_p.at[j], first)
        late_store(late_p.at[j], 0, PIECE, 8 + PIECE * j)

    def pass_on(i):
        arrival(1, 0, i).wait_recv()
        forward(0, i).start()
        partner_copy(2, 0, i).start()
        arrival(0, 1, i).wait_recv()
        forward(1, i).start()
        partner_copy(1, 1, i).start()
        arrival(0, 0, i).wait_recv()
        partner_copy(1, 0, i).start()
        arrival(1, 1, i).wait_recv()
        partner_copy(2, 1, i).start()

    each(pass_on)

    for copy in late_copies:
        copy.wait()

    def finish_own(i):
        for h in HALVES:
            own_store(h, i).wait()
            arrival(2, h, i).wait_recv()
            for n in range(3):
                own_copy(n, h, i).wait_send()

    each(finish_own)

    def finish(i):
        for h in HALVES:
            forward(h, i).wait_send()
            partner_copy(3, h, i).wait_send()
            partner_arrival(3, h, i).wait_recv()

    def pass_last(i):
        for h in HALVES:
            forward_arrival(h, i).wait_recv()
            partner_copy(3, h, i).start()
            for q in (1, 2):
                partner_copy(q, h, i).wait_send()
                partner_arrival(q, h, i).wait_recv()
        if isinstance(i, int):
            finish(i - 1)
        else:
            pl.when(i > 0)(lambda: finish(i - 1))

    each(pass_last)
    finish(HALF - 1)


def gather_params(g, m, v, p, norm, lr):
    buf = pltpu.VMEM((2, PIECE, LANES), F32)
    pairs = DMA((2, HALF))
    triples = DMA((3, 2, HALF))
    return pl.pallas_call(
        gather_kernel,
        name="gather_params",
        out_shape=[jax.ShapeDtypeStruct((FLAT_ROWS, 1, LANES), F32), jax.ShapeDtypeStruct((LATE_HALF, 1, LANES), F32), jax.ShapeDtypeStruct((LATE_HALF, 1, LANES), F32)],
        in_specs=[ANY] * 4 + [VMEM_SPEC, SMEM_SPEC],
        out_specs=[ANY] * 3,
        scratch_shapes=[buf, buf, buf, buf, pltpu.VMEM((2, HALF, PIECE, LANES), F32), pltpu.VMEM((LATE_END - LATE_FIRST, PIECE, LANES), F32),
                        DMA((4, 2)), pairs, DMA((LATE_END - LATE_FIRST + 4,)), triples, triples, pairs, pairs, triples, triples],
        compiler_params=pltpu.CompilerParams(collective_id=1, has_side_effects=True, vmem_limit_bytes=VMEM_LIMIT),
        cost_estimate=COST,
    )(g, m, v, p, norm, lr)


def state_kernel(g, m, v, p, norm, lr, new_p, new_m, new_v, norm_out, gb, mb, vb, pb, pn, mn, vn, in_sem, out_sem):
    me = lax.axis_index("dp")
    norm_row = norm[pl.ds(0, 1), :]
    norm_out[0] = jnp.max(norm[...])

    def window(i):
        rows = STATE_LAST if isinstance(i, int) and i == STATE_COUNT else STATE_ROWS
        slot = lax.rem(i, STATE_SLOTS)
        return slot, pl.ds(pl.multiple_of(i * STATE_ROWS, 8), rows), pl.ds(0, rows)

    def loads(i):
        slot, rows, size = window(i)
        pairs = ((g.at[rows, 0], gb), (m.at[rows], mb), (v.at[rows], vb), (p.at[rows], pb))
        return [pltpu.make_async_copy(src, buf.at[slot, size], in_sem.at[n, slot]) for n, (src, buf) in enumerate(pairs)]

    def stores(i):
        slot, rows, size = window(i)
        pairs = ((pn, new_p), (mn, new_m), (vn, new_v))
        return [pltpu.make_async_copy(buf.at[slot, size], dst.at[rows], out_sem.at[n, slot]) for n, (buf, dst) in enumerate(pairs)]

    def run(copies, wait=False):
        for copy in copies:
            copy.wait() if wait else copy.start()

    def compute(i):
        slot = lax.rem(i, STATE_SLOTS)

        @pl.loop(0, STATE_ROWS // SUB)
        def _(s):
            start = pl.multiple_of(s * SUB, 8)
            rows = pl.ds(start, SUB)
            pn[slot, rows], mn[slot, rows], vn[slot, rows] = adam_rows(
                gb[slot, rows], mb[slot, rows], vb[slot, rows], pb[slot, rows], norm_row, lr[0],
                decay_rows(me, i * STATE_ROWS + start, SUB))

    for i in range(STATE_SLOTS):
        run(loads(i))

    @pl.loop(0, STATE_COUNT)
    def _(i):
        run(loads(i), wait=True)

        @pl.when(i >= STATE_SLOTS)
        def _():
            run(stores(i - STATE_SLOTS), wait=True)

        compute(i)
        run(stores(i))

        @pl.when(i + STATE_SLOTS < STATE_COUNT)
        def _():
            run(loads(i + STATE_SLOTS))

        @pl.when(i + STATE_SLOTS == STATE_COUNT)
        def _():
            run(loads(STATE_COUNT))

    run(loads(STATE_COUNT), wait=True)
    run(stores(STATE_COUNT - STATE_SLOTS), wait=True)
    compute(STATE_COUNT)
    run(stores(STATE_COUNT))
    for n in range(STATE_SLOTS):
        run(stores(STATE_COUNT - STATE_SLOTS + 1 + n), wait=True)


def new_state(g, m, v, p, norm, lr):
    return pl.pallas_call(
        state_kernel,
        name="new_state",
        out_shape=[jax.ShapeDtypeStruct((SEG, LANES), F32)] * 3 + [jax.ShapeDtypeStruct((1,), F32)],
        in_specs=[ANY] * 4 + [VMEM_SPEC, SMEM_SPEC],
        out_specs=[ANY] * 3 + [SMEM_SPEC],
        scratch_shapes=[pltpu.VMEM((STATE_SLOTS, STATE_ROWS, LANES), F32)] * 7 + [DMA((4, STATE_SLOTS)), DMA((3, STATE_SLOTS))],
        compiler_params=pltpu.CompilerParams(vmem_limit_bytes=VMEM_LIMIT),
        cost_estimate=COST,
    )(g, m, v, p, norm, lr)


def solution(mesh):
    def local_step(*arrays):
        grads = [a.reshape(r, w * LANES) for a, r, w in zip(arrays[:7], NAMES_ROWS, WIDTHS)]
        norms = [a.reshape(s) for a, s in zip(arrays[7:10], GAINS)]
        master, exp_avg, exp_avg_sq = [a.reshape(SEG, LANES) for a in arrays[10:13]]
        lr = arrays[13].reshape(1)
        g, norm = reduce_grads(grads, norms)
        full, *late = gather_params(g, exp_avg, exp_avg_sq, master, norm, lr)

        def permute(a, bits):
            return lax.ppermute(a, "dp", [(d, d ^ bits) for d in range(NDEV)])

        by_y, by_x = permute(late[0], 4), permute(late[1], 2)
        far_x, far_y = permute(late[0], 2), permute(late[1], 4)
        own = [permute(a, 1) for a in late]
        state = list(new_state(g, exp_avg, exp_avg_sq, master, norm, lr))
        by_y, by_x, full, state[0] = lax.optimization_barrier((by_y, by_x, full, state[0]))
        across_y = permute(by_y, 2)
        across_x = permute(by_x, 4)
        across = across_y, across_x
        from_y, from_x = permute(by_y, 1), permute(by_x, 1)
        wide, down, small = (4, 5), (3, 6), (0, 1, 2)
        params = dict(zip(wide, unpack_early(full, wide, [])))
        far_x, far_y, full, params[4] = lax.optimization_barrier((far_x, far_y, full, params[4]))
        far = permute(far_x, 1), permute(far_y, 1)
        params |= dict(zip(down, unpack_early(full, down, [])))
        lates = dict(enumerate([late, own, (far_x, by_x), (far[0], from_x), (by_y, far_y), (from_y, far[1])]))
        params = unpack_late(full, lates, params)
        *across, full, params[6] = lax.optimization_barrier((*across, full, params[6]))
        from_across = [permute(a, 1) for a in across]
        rest = list(unpack_early(full, small, GAINS[:2] + [(D,)]))
        params |= dict(zip(small, rest))
        params = unpack_late(full, {6: across, 7: from_across}, params)
        params = [params[t] for t in TENSORS] + rest[len(small):]
        shapes = SHAPES + GAINS[:2] + [(D,)]
        return tuple([a.reshape(-1) for a in state[:3]] + [a.reshape(s) for a, s in zip(params, shapes)] + [state[3].reshape(())])

    return jax.shard_map(local_step, mesh=mesh, in_specs=(P("dp"),) * 13 + (P(),), out_specs=(P("dp"),) * 3 + (P(),) * 11, check_vma=False)
```

profile of v0, /device:TPU:0, one launch (start us, length us, event | category | flops | bytes accessed | tf_op | source)
XLA Modules:
  0.0 1022.2 jit_solution(15471375846836065657)
XLA Ops:
  1.3 503.9 %reduce_grads.1 = (f32[29125,1,128]{2,1,0:T(1,128)}, f32[8,128]{1,0:T(8,128)}, f32[4,4,2,2,4860,1,128]{6,5,4,3,2,1,0:T(1,128)}, f32[4,2,16,911,1,128]{5,4,3,2,1,...) custom-call(bf16[1792,896]{1,0:T(8,128)(2,1)} %bitcast.39, bf16[1792,128]{1,0:T(8,128)(2,1)} %bitcast.41, ...), custom_call_target="tpu_custom_call" | custom-call | flops 200000000 | bytes 100000000 | tf_op jit(solution)/shard_map/reduce_grads/pallas_call | solution.py:507
  505.2 399.7 %gather_params.1 = (f32[233000,1,128]{2,1,0:T(1,128)}, f32[2752,1,128]{2,1,0:T(1,128)}, f32[2752,1,128]{2,1,0:T(1,128)}) custom-call(f32[29125,1,128]{2,1,0:T(1,128)} %get-tuple-element.53.g, f32[29125,128]{1,0:T(8,128)} %bitcast.29, f32[29125,128]{1,0:T(8,128)} %bitcast.31, f32[29125,128]{1,0:T(8,128)} %bitcast.33, f32[8,128]{1,0:T(8,128)} %get-tuple-element.54.norm, ...), custom_call_target="tpu_custom_call" | custom-call | flops 200000000 | bytes 100000000 | tf_op jit(solution)/shard_map/gather_params/pallas_call | solution.py:724
  904.9 1.7 collective-permute-start
  906.6 1.5 collective-permute-start.1
  908.0 0.6 collective-permute-start.4
  908.6 0.4 collective-permute-start.5
  909.0 0.0 collective-permute-start.6
  909.0 36.0 %new_state.1 = (f32[29125,128]{1,0:T(8,128)}, f32[29125,128]{1,0:T(8,128)}, f32[29125,128]{1,0:T(8,128)}, f32[1]{0:T(128)}) custom-call(f32[29125,1,128]{2,1,0:T(1,128)} %get-tuple-element.53.g, f32[29125,128]{1,0:T(8,128)} %bitcast.30, f32[29125,128]{1,0:T(8,128)} %bitcast.32, f32[29125,128]{1,0:T(8,128)} %bitcast.34, f32[8,128]{1,0:T(8,128)} %get-tuple-element.54.norm, ...), custom_call_target="tpu_custom_call" | custom-call | flops 200000000 | bytes 100000000 | tf_op jit(solution)/shard_map/new_state/pallas_call | solution.py:803
  945.0 0.0 collective-permute-done.refs_8_
  945.0 0.5 collective-permute-start.7
  945.5 0.0 collective-permute-done.1.refs_5_
  945.5 28.4 %unpack_early.3 = (bf16[1792,4864]{1,0:T(8,128)(2,1)}, bf16[1792,4864]{1,0:T(8,128)(2,1)}) custom-call(f32[233000,1,128]{2,1,0:T(1,128)} %get-tuple-element.74.flat), custom_call_target="tpu_custom_call" | custom-call | flops 200000000 | bytes 100000000 | tf_op jit(solution)/shard_map/unpack_early/pallas_call | solution.py:201
  973.9 0.0 collective-permute-done.4.refs_4_
  973.9 0.0 collective-permute-done.5.refs_9_
  973.9 0.0 collective-permute-start.11
  973.9 0.5 collective-permute-start.8
  974.4 0.0 collective-permute-start.10
  974.5 0.0 collective-permute-done.6.refs_2_
  974.5 0.5 collective-permute-start.9
  975.0 0.0 collective-permute-done.7.refs_3_
  975.0 1.7 collective-permute-start.2
  976.7 0.8 collective-permute-done.11.refs_11_
  977.4 1.6 collective-permute-start.3
  979.1 16.6 %unpack_early.4 = (bf16[1792,896]{1,0:T(8,128)(2,1)}, bf16[9728,896]{1,0:T(8,128)(2,1)}) custom-call(f32[233000,1,128]{2,1,0:T(1,128)} %get-tuple-element.74.flat), custom_call_target="tpu_custom_call" | custom-call | flops 200000000 | bytes 100000000 | tf_op jit(solution)/shard_map/unpack_early/pallas_call | solution.py:201
  995.7 0.0 collective-permute-done.8.refs_6_
  995.7 0.0 collective-permute-done.10.refs_10_
  995.7 0.0 collective-permute-done.9.refs_7_
  995.8 10.2 unpack_late.2
  1005.9 2.2 collective-permute-done.2.refs_0_
  1008.1 2.6 collective-permute-done.3.refs_1_
  1010.7 0.0 collective-permute-start.12
  1010.7 0.5 collective-permute-start.13
  1011.2 6.7 unpack_early.5
  1017.9 0.0 collective-permute-done.12.refs_2_
  1017.9 0.0 collective-permute-done.13.refs_3_
  1017.9 4.3 unpack_late.3
Async XLA Ops:
  904.9 40.1 %collective-permute-start = (f32[2752,1,128]{2,1,0:T(1,128)}, f32[2752,1,128]{2,1,0:T(1,128)}, u32[]{:S(2)}, u32[]{:S(2)}) collective-permute-start(f32[2752,1,128]{2,1,0:T(1,128)} %get-tuple-element.55.refs_0_), channel_id=1, source_target_pairs={{0,4},{1,5},{2,6},{3,7},{4,0},{5,1},{6,2},{7,3}} | collective-permute-start | bytes 4227080 | tf_op jit(solution)/shard_map/ppermute | solution.py:825
  906.6 38.9 %collective-permute-start.1 = (f32[2752,1,128]{2,1,0:T(1,128)}, f32[2752,1,128]{2,1,0:T(1,128)}, u32[]{:S(2)}, u32[]{:S(2)}) collective-permute-start(f32[2752,1,128]{2,1,0:T(1,128)} %get-tuple-element.56.refs_1_), channel_id=1, source_target_pairs={{0,2},{1,3},{2,0},{3,1},{4,6},{5,7},{6,4},{7,5}} | collective-permute-start | bytes 4227080 | tf_op jit(solution)/shard_map/ppermute | solution.py:825
  908.0 65.8 %collective-permute-start.4 = (f32[2752,1,128]{2,1,0:T(1,128)}, f32[2752,1,128]{2,1,0:T(1,128)}, u32[]{:S(2)}, u32[]{:S(2)}) collective-permute-start(f32[2752,1,128]{2,1,0:T(1,128)} %get-tuple-element.55.refs_0_), channel_id=1, source_target_pairs={{0,2},{1,3},{2,0},{3,1},{4,6},{5,7},{6,4},{7,5}} | collective-permute-start | bytes 4227080 | tf_op jit(solution)/shard_map/ppermute | solution.py:825
  908.6 65.3 %collective-permute-start.5 = (f32[2752,1,128]{2,1,0:T(1,128)}, f32[2752,1,128]{2,1,0:T(1,128)}, u32[]{:S(2)}, u32[]{:S(2)}) collective-permute-start(f32[2752,1,128]{2,1,0:T(1,128)} %get-tuple-element.56.refs_1_), channel_id=1, source_target_pairs={{0,4},{1,5},{2,6},{3,7},{4,0},{5,1},{6,2},{7,3}} | collective-permute-start | bytes 4227080 | tf_op jit(solution)/shard_map/ppermute | solution.py:825
  909.0 65.5 %collective-permute-start.6 = (f32[2752,1,128]{2,1,0:T(1,128)}, f32[2752,1,128]{2,1,0:T(1,128)}, u32[]{:S(2)}, u32[]{:S(2)}) collective-permute-start(f32[2752,1,128]{2,1,0:T(1,128)} %get-tuple-element.55.refs_0_), channel_id=1, source_target_pairs={{0,1},{1,0},{2,3},{3,2},{4,5},{5,4},{6,7},{7,6}} | collective-permute-start | bytes 4227080 | tf_op jit(solution)/shard_map/ppermute | solution.py:825
  945.0 30.0 %collective-permute-start.7 = (f32[2752,1,128]{2,1,0:T(1,128)}, f32[2752,1,128]{2,1,0:T(1,128)}, u32[]{:S(2)}, u32[]{:S(2)}) collective-permute-start(f32[2752,1,128]{2,1,0:T(1,128)} %get-tuple-element.56.refs_1_), channel_id=1, source_target_pairs={{0,1},{1,0},{2,3},{3,2},{4,5},{5,4},{6,7},{7,6}} | collective-permute-start | bytes 4227080 | tf_op jit(solution)/shard_map/ppermute | solution.py:825
  973.9 3.5 collective-permute-start.11
  973.9 21.8 %collective-permute-start.8 = (f32[2752,1,128]{2,1,0:T(1,128)}, f32[2752,1,128]{2,1,0:T(1,128)}, u32[]{:S(2)}, u32[]{:S(2)}) collective-permute-start(f32[2752,1,128]{2,1,0:T(1,128)} %collective-permute-done.4.refs_4_), channel_id=1, source_target_pairs={{0,1},{1,0},{2,3},{3,2},{4,5},{5,4},{6,7},{7,6}} | collective-permute-start | bytes 4227080 | tf_op jit(solution)/shard_map/ppermute | solution.py:825
  974.4 21.3 %collective-permute-start.10 = (f32[2752,1,128]{2,1,0:T(1,128)}, f32[2752,1,128]{2,1,0:T(1,128)}, u32[]{:S(2)}, u32[]{:S(2)}) collective-permute-start(f32[2752,1,128]{2,1,0:T(1,128)} %collective-permute-done.refs_8_), channel_id=1, source_target_pairs={{0,1},{1,0},{2,3},{3,2},{4,5},{5,4},{6,7},{7,6}} | collective-permute-start | bytes 4227080 | tf_op jit(solution)/shard_map/ppermute | solution.py:825
  974.5 21.3 %collective-permute-start.9 = (f32[2752,1,128]{2,1,0:T(1,128)}, f32[2752,1,128]{2,1,0:T(1,128)}, u32[]{:S(2)}, u32[]{:S(2)}) collective-permute-start(f32[2752,1,128]{2,1,0:T(1,128)} %collective-permute-done.1.refs_5_), channel_id=1, source_target_pairs={{0,1},{1,0},{2,3},{3,2},{4,5},{5,4},{6,7},{7,6}} | collective-permute-start | bytes 4227080 | tf_op jit(solution)/shard_map/ppermute | solution.py:825
  975.0 33.1 %collective-permute-start.2 = (f32[2752,1,128]{2,1,0:T(1,128)}, f32[2752,1,128]{2,1,0:T(1,128)}, u32[]{:S(2)}, u32[]{:S(2)}) collective-permute-start(f32[2752,1,128]{2,1,0:T(1,128)} %collective-permute-done.refs_8_), channel_id=1, source_target_pairs={{0,2},{1,3},{2,0},{3,1},{4,6},{5,7},{6,4},{7,5}} | collective-permute-start | bytes 4227080 | tf_op jit(solution)/shard_map/ppermute | solution.py:825
  977.4 33.2 %collective-permute-start.3 = (f32[2752,1,128]{2,1,0:T(1,128)}, f32[2752,1,128]{2,1,0:T(1,128)}, u32[]{:S(2)}, u32[]{:S(2)}) collective-permute-start(f32[2752,1,128]{2,1,0:T(1,128)} %collective-permute-done.1.refs_5_), channel_id=1, source_target_pairs={{0,4},{1,5},{2,6},{3,7},{4,0},{5,1},{6,2},{7,3}} | collective-permute-start | bytes 4227080 | tf_op jit(solution)/shard_map/ppermute | solution.py:825
  1010.7 7.2 collective-permute-start.12
  1010.7 7.2 collective-permute-start.13
where the time goes:
time: 1030 us; the launch traced here: 1020 us
  Pallas kernels  1010 us (98%)
    pallas_call x1, Pallas kernels, reduce_grads(): pl.pallas_call(reduce_kernel, name='reduce_grads', out_shape=[jax.ShapeDt...  504 us
    pallas_call x1, Pallas kernels, gather_params(): pl.pallas_call(gather_kernel, name='gather_params', out_shape=[jax.ShapeD...  400 us
    pallas_call x3, Pallas kernels, unpack_early(): pl.pallas_call(functools.partial(unpack_early_kernel, tensors), name='unp...  51.6 us
    pallas_call x1, Pallas kernels, new_state(): pl.pallas_call(state_kernel, name='new_state', out_shape=[jax.ShapeDtypeS...  36 us
  transfers between devices with their start and end apart: 14, of which 3 were waited for; matrix products, arithmetic and copies ran while one was open for 0% of the time, Pallas kernels for 10%

commit v1 on v0

--- a/solution.py
+++ b/solution.py
@@ -66,9 +66,9 @@
     return max(g for g in GROUPS[width] if rows % g == 0)
 
 
-PIECE = 912
-PIECES = 32
-LATE_FIRST, LATE_END = 25, 31
+PIECE = 608
+PIECES = 48
+LATE_FIRST, LATE_END = 37, 47
 LATE_ROWS = PIECE * (LATE_END - LATE_FIRST) + 16
 PIECE_LAST = SEG - (PIECES - 1) * PIECE
 HALF = (PIECES - LATE_END + LATE_FIRST) // 2
@@ -529,7 +529,7 @@
     return p - lr * (decay_term + adam_dir), new_m, new_v
 
 
-STATE_ROWS = PIECE
+STATE_ROWS = 912
 STATE_COUNT = SEG // STATE_ROWS
 STATE_LAST = SEG - STATE_COUNT * STATE_ROWS
 STATE_SLOTS = 4

time: 1030 us -> 1020 us (level)
  Pallas kernels: 1010 us -> 996 us
  transfers between devices with their start and end apart: 14 -> 14, of which waited for: 3 -> 4; matrix products, arithmetic and copies ran while one was open for 0% -> 0% of each run, Pallas kernels for 10% -> 10%
where the time goes in v1:
time: 1020 us
  Pallas kernels  996 us (98%)
  waiting for transfers between devices  13.8 us (1%)
    pallas_call x1, Pallas kernels, reduce_grads(): pl.pallas_call(reduce_kernel, name='reduce_grads', out_shape=[jax.ShapeDt...  504 us
    pallas_call x1, Pallas kernels, gather_params(): pl.pallas_call(gather_kernel, name='gather_params', out_shape=[jax.ShapeD...  391 us
    pallas_call x3, Pallas kernels, unpack_early(): pl.pallas_call(functools.partial(unpack_early_kernel, tensors), name='unp...  49.8 us
    pallas_call x1, Pallas kernels, new_state(): pl.pallas_call(state_kernel, name='new_state', out_shape=[jax.ShapeDtypeS...  36 us
  transfers between devices with their start and end apart: 14, of which 4 were waited for; matrix products, arithmetic and copies ran while one was open for 0% of the time, Pallas kernels for 10%

profile of v1, /device:TPU:0, one launch (start us, length us, event | category | flops | bytes accessed | tf_op | source)
XLA Modules:
  0.0 1019.7 jit_solution(1512461514098112026)
XLA Ops:
  1.3 503.9 %reduce_grads.1 = (f32[29125,1,128]{2,1,0:T(1,128)}, f32[8,128]{1,0:T(8,128)}, f32[4,4,2,2,4860,1,128]{6,5,4,3,2,1,0:T(1,128)}, f32[4,2,16,911,1,128]{5,4,3,2,1,...) custom-call(bf16[1792,896]{1,0:T(8,128)(2,1)} %bitcast.39, bf16[1792,128]{1,0:T(8,128)(2,1)} %bitcast.41, ...), custom_call_target="tpu_custom_call" | custom-call | flops 200000000 | bytes 100000000 | tf_op jit(solution)/shard_map/reduce_grads/pallas_call | solution.py:507
  505.2 390.7 %gather_params.1 = (f32[233000,1,128]{2,1,0:T(1,128)}, f32[3056,1,128]{2,1,0:T(1,128)}, f32[3056,1,128]{2,1,0:T(1,128)}) custom-call(f32[29125,1,128]{2,1,0:T(1,128)} %get-tuple-element.53.g, f32[29125,128]{1,0:T(8,128)} %bitcast.29, f32[29125,128]{1,0:T(8,128)} %bitcast.31, f32[29125,128]{1,0:T(8,128)} %bitcast.33, f32[8,128]{1,0:T(8,128)} %get-tuple-element.54.norm, ...), custom_call_target="tpu_custom_call" | custom-call | flops 200000000 | bytes 100000000 | tf_op jit(solution)/shard_map/gather_params/pallas_call | solution.py:724
  895.9 1.5 collective-permute-start
  897.4 1.5 collective-permute-start.1
  898.9 0.6 collective-permute-start.4
  899.4 0.6 collective-permute-start.5
  900.0 0.0 collective-permute-start.6
  900.0 36.0 %new_state.1 = (f32[29125,128]{1,0:T(8,128)}, f32[29125,128]{1,0:T(8,128)}, f32[29125,128]{1,0:T(8,128)}, f32[1]{0:T(128)}) custom-call(f32[29125,1,128]{2,1,0:T(1,128)} %get-tuple-element.53.g, f32[29125,128]{1,0:T(8,128)} %bitcast.30, f32[29125,128]{1,0:T(8,128)} %bitcast.32, f32[29125,128]{1,0:T(8,128)} %bitcast.34, f32[8,128]{1,0:T(8,128)} %get-tuple-element.54.norm, ...), custom_call_target="tpu_custom_call" | custom-call | flops 200000000 | bytes 100000000 | tf_op jit(solution)/shard_map/new_state/pallas_call | solution.py:803
  936.0 0.0 collective-permute-done.refs_8_
  936.0 0.5 collective-permute-start.7
  936.5 0.0 collective-permute-done.1.refs_5_
  936.5 28.1 %unpack_early.3 = (bf16[1792,4864]{1,0:T(8,128)(2,1)}, bf16[1792,4864]{1,0:T(8,128)(2,1)}) custom-call(f32[233000,1,128]{2,1,0:T(1,128)} %get-tuple-element.74.flat), custom_call_target="tpu_custom_call" | custom-call | flops 200000000 | bytes 100000000 | tf_op jit(solution)/shard_map/unpack_early/pallas_call | solution.py:201
  964.7 2.8 collective-permute-done.4.refs_4_
  967.5 0.0 collective-permute-done.5.refs_9_
  967.5 0.0 collective-permute-start.11
  967.5 0.5 collective-permute-start.8
  968.0 0.0 collective-permute-start.10
  968.0 0.0 collective-permute-done.6.refs_2_
  968.0 0.5 collective-permute-start.9
  968.5 0.0 collective-permute-done.7.refs_3_
  968.5 1.5 collective-permute-start.2
  970.0 1.2 collective-permute-done.11.refs_11_
  971.2 0.6 collective-permute-start.3
  971.8 15.0 %unpack_early.4 = (bf16[1792,896]{1,0:T(8,128)(2,1)}, bf16[9728,896]{1,0:T(8,128)(2,1)}) custom-call(f32[233000,1,128]{2,1,0:T(1,128)} %get-tuple-element.74.flat), custom_call_target="tpu_custom_call" | custom-call | flops 200000000 | bytes 100000000 | tf_op jit(solution)/shard_map/unpack_early/pallas_call | solution.py:201
  986.8 0.0 collective-permute-done.8.refs_6_
  986.8 0.0 collective-permute-done.10.refs_10_
  986.8 0.0 collective-permute-done.9.refs_7_
  986.9 11.1 %unpack_late.2 = (bf16[1792,896]{1,0:T(8,128)(2,1)}, bf16[1792,4864]{1,0:T(8,128)(2,1)}, bf16[1792,4864]{1,0:T(8,128)(2,1)}, bf16[9728,896]{1,0:T(8,128)(2,1)}) custom-call(f32[233000,1,128]{2,1,0:T(1,128)} %get-tuple-element.74.flat, ...), custom_call_target="tpu_custom_call", output_to_operand_aliasing={{0}: (13, {}), {1}: (14, {}), {2}: (15, {}), {3}: (16, {})} | custom-call | flops 200000000 | bytes 100000000 | tf_op jit(solution)/shard_map/unpack_late/pallas_call | solution.py:231
  998.0 7.0 collective-permute-done.2.refs_0_
  1005.0 2.8 collective-permute-done.3.refs_1_
  1007.8 0.0 collective-permute-start.12
  1007.8 0.5 collective-permute-start.13
  1008.3 6.7 unpack_early.5
  1015.0 0.0 collective-permute-done.12.refs_2_
  1015.0 0.0 collective-permute-done.13.refs_3_
  1015.0 4.7 unpack_late.3
Async XLA Ops:
  895.9 40.1 %collective-permute-start = (f32[3056,1,128]{2,1,0:T(1,128)}, f32[3056,1,128]{2,1,0:T(1,128)}, u32[]{:S(2)}, u32[]{:S(2)}) collective-permute-start(f32[3056,1,128]{2,1,0:T(1,128)} %get-tuple-element.55.refs_0_), channel_id=1, source_target_pairs={{0,4},{1,5},{2,6},{3,7},{4,0},{5,1},{6,2},{7,3}} | collective-permute-start | bytes 4694024 | tf_op jit(solution)/shard_map/ppermute | solution.py:825
  897.4 39.1 %collective-permute-start.1 = (f32[3056,1,128]{2,1,0:T(1,128)}, f32[3056,1,128]{2,1,0:T(1,128)}, u32[]{:S(2)}, u32[]{:S(2)}) collective-permute-start(f32[3056,1,128]{2,1,0:T(1,128)} %get-tuple-element.56.refs_1_), channel_id=1, source_target_pairs={{0,2},{1,3},{2,0},{3,1},{4,6},{5,7},{6,4},{7,5}} | collective-permute-start | bytes 4694024 | tf_op jit(solution)/shard_map/ppermute | solution.py:825
  898.9 68.6 %collective-permute-start.4 = (f32[3056,1,128]{2,1,0:T(1,128)}, f32[3056,1,128]{2,1,0:T(1,128)}, u32[]{:S(2)}, u32[]{:S(2)}) collective-permute-start(f32[3056,1,128]{2,1,0:T(1,128)} %get-tuple-element.55.refs_0_), channel_id=1, source_target_pairs={{0,2},{1,3},{2,0},{3,1},{4,6},{5,7},{6,4},{7,5}} | collective-permute-start | bytes 4694024 | tf_op jit(solution)/shard_map/ppermute | solution.py:825
  899.4 68.0 %collective-permute-start.5 = (f32[3056,1,128]{2,1,0:T(1,128)}, f32[3056,1,128]{2,1,0:T(1,128)}, u32[]{:S(2)}, u32[]{:S(2)}) collective-permute-start(f32[3056,1,128]{2,1,0:T(1,128)} %get-tuple-element.56.refs_1_), channel_id=1, source_target_pairs={{0,4},{1,5},{2,6},{3,7},{4,0},{5,1},{6,2},{7,3}} | collective-permute-start | bytes 4694024 | tf_op jit(solution)/shard_map/ppermute | solution.py:825
  900.0 68.0 %collective-permute-start.6 = (f32[3056,1,128]{2,1,0:T(1,128)}, f32[3056,1,128]{2,1,0:T(1,128)}, u32[]{:S(2)}, u32[]{:S(2)}) collective-permute-start(f32[3056,1,128]{2,1,0:T(1,128)} %get-tuple-element.55.refs_0_), channel_id=1, source_target_pairs={{0,1},{1,0},{2,3},{3,2},{4,5},{5,4},{6,7},{7,6}} | collective-permute-start | bytes 4694024 | tf_op jit(solution)/shard_map/ppermute | solution.py:825
  936.0 32.5 %collective-permute-start.7 = (f32[3056,1,128]{2,1,0:T(1,128)}, f32[3056,1,128]{2,1,0:T(1,128)}, u32[]{:S(2)}, u32[]{:S(2)}) collective-permute-start(f32[3056,1,128]{2,1,0:T(1,128)} %get-tuple-element.56.refs_1_), channel_id=1, source_target_pairs={{0,1},{1,0},{2,3},{3,2},{4,5},{5,4},{6,7},{7,6}} | collective-permute-start | bytes 4694024 | tf_op jit(solution)/shard_map/ppermute | solution.py:825
  967.5 3.7 collective-permute-start.11
  967.5 19.4 %collective-permute-start.8 = (f32[3056,1,128]{2,1,0:T(1,128)}, f32[3056,1,128]{2,1,0:T(1,128)}, u32[]{:S(2)}, u32[]{:S(2)}) collective-permute-start(f32[3056,1,128]{2,1,0:T(1,128)} %collective-permute-done.4.refs_4_), channel_id=1, source_target_pairs={{0,1},{1,0},{2,3},{3,2},{4,5},{5,4},{6,7},{7,6}} | collective-permute-start | bytes 4694024 | tf_op jit(solution)/shard_map/ppermute | solution.py:825
  968.0 18.9 %collective-permute-start.10 = (f32[3056,1,128]{2,1,0:T(1,128)}, f32[3056,1,128]{2,1,0:T(1,128)}, u32[]{:S(2)}, u32[]{:S(2)}) collective-permute-start(f32[3056,1,128]{2,1,0:T(1,128)} %collective-permute-done.refs_8_), channel_id=1, source_target_pairs={{0,1},{1,0},{2,3},{3,2},{4,5},{5,4},{6,7},{7,6}} | collective-permute-start | bytes 4694024 | tf_op jit(solution)/shard_map/ppermute | solution.py:825
  968.0 18.9 %collective-permute-start.9 = (f32[3056,1,128]{2,1,0:T(1,128)}, f32[3056,1,128]{2,1,0:T(1,128)}, u32[]{:S(2)}, u32[]{:S(2)}) collective-permute-start(f32[3056,1,128]{2,1,0:T(1,128)} %collective-permute-done.1.refs_5_), channel_id=1, source_target_pairs={{0,1},{1,0},{2,3},{3,2},{4,5},{5,4},{6,7},{7,6}} | collective-permute-start | bytes 4694024 | tf_op jit(solution)/shard_map/ppermute | solution.py:825
  968.5 36.5 %collective-permute-start.2 = (f32[3056,1,128]{2,1,0:T(1,128)}, f32[3056,1,128]{2,1,0:T(1,128)}, u32[]{:S(2)}, u32[]{:S(2)}) collective-permute-start(f32[3056,1,128]{2,1,0:T(1,128)} %collective-permute-done.refs_8_), channel_id=1, source_target_pairs={{0,2},{1,3},{2,0},{3,1},{4,6},{5,7},{6,4},{7,5}} | collective-permute-start | bytes 4694024 | tf_op jit(solution)/shard_map/ppermute | solution.py:825
  971.2 36.6 %collective-permute-start.3 = (f32[3056,1,128]{2,1,0:T(1,128)}, f32[3056,1,128]{2,1,0:T(1,128)}, u32[]{:S(2)}, u32[]{:S(2)}) collective-permute-start(f32[3056,1,128]{2,1,0:T(1,128)} %collective-permute-done.1.refs_5_), channel_id=1, source_target_pairs={{0,4},{1,5},{2,6},{3,7},{4,0},{5,1},{6,2},{7,3}} | collective-permute-start | bytes 4694024 | tf_op jit(solution)/shard_map/ppermute | solution.py:825
  1007.8 7.2 collective-permute-start.12
  1007.8 7.2 collective-permute-start.13
